TPU v7x, 32 devices: a whole 2x2x4 slice. The times are simulated.
32 devices in a mesh: leaf: 2 (over core), row: 4 (over y, x), col: 4 (over z).
Axes of the slice: x: 2, y: 2, z: 4, core: 2. Of those that a mesh axis runs over, the one named last changes fastest.
Arguments:
- rhs_leaf: bfloat16 [2, 8, 64, 2048], P('leaf', None, None, 'col'), may hold values from -6 to 6
- dinv_leaf: bfloat16 [2, 8, 2048, 2048], P('leaf', None, 'row', 'col'), as said below
- panel_leaf: bfloat16 [2, 8, 1024, 2048], P('leaf', None, 'col', 'row'), may hold values from -0.0625 to 0.0625
- counts: int32 [2, 8], P('leaf'), may hold values from 256 to 2048, as said below
- row_index: int32 [2, 8, 1024], P('leaf'), may hold values from 0 to 4095, as said below
- rhs_root: bfloat16 [64, 4096], P(None, 'col'), may hold values from -6 to 6
- dinv_root: bfloat16 [4096, 4096], P(('leaf', 'row')), as said below
Outputs:
- y_leaf: bfloat16 [2, 8, 64, 2048], P('leaf', None, None, 'row')
- y_root: bfloat16 [64, 4096], P(None, ('leaf', 'row'))
Inputs may be any that keep to these rules, and one draw needn't show every extreme that they name: `counts`: each subtree supernode has at least 256 columns; at least one supernode of every draw has all 2048. `row_index`: within one supernode the 1024 entries are distinct and increasing. `dinv_leaf`: each [2048, 2048] block is lower triangular with a nonzero diagonal. `dinv_root`: lower triangular with a nonzero diagonal.
All inputs are finite; a program needn't handle non-finite values.
Results may differ from a plain program's by a relative error of at most 0.0053.
Values may be sent and summed in bfloat16 or wider, within the bound.
No kernel may reach another device: no remote copies, remote signals or barrier semaphores. Data moves between devices by JAX's collectives and lax.ppermute only.
A program may use at most 64 MiB of HBM per device.

v0:
```python
import jax
import jax.numpy as jnp
from jax import lax
from jax.sharding import PartitionSpec as P


def local(rhs_leaf, dinv_leaf, panel_leaf, counts, row_index, rhs_root, dinv_root):
    width_col = rhs_leaf.shape[3]
    width_row = dinv_leaf.shape[2]
    panel_rows = panel_leaf.shape[2]
    columns = rhs_root.shape[0]
    sep_width = rhs_root.shape[1] * lax.axis_size("col")
    limit = counts[0][:, None, None]
    col_slots = lax.axis_index("col") * width_col + lax.iota(jnp.int32, width_col)
    masked = jnp.where(col_slots[None, None, :] < limit, rhs_leaf[0], jnp.zeros((), jnp.bfloat16))
    partial_value = jnp.einsum(
        "kbj,kij->kbi", masked, dinv_leaf[0], preferred_element_type=jnp.float32
    )
    summed = lax.psum(partial_value, "col")
    row_slots = lax.axis_index("row") * width_row + lax.iota(jnp.int32, width_row)
    live_rows = (row_slots[None, None, :] < limit).astype(jnp.float32)
    solved = (summed * live_rows).astype(jnp.bfloat16)
    update = jnp.einsum("kbi,kri->kbr", solved, panel_leaf[0], preferred_element_type=jnp.float32)
    offset = lax.axis_index("col") * panel_rows
    targets = lax.dynamic_slice_in_dim(row_index[0], offset, panel_rows, 1)
    flat_update = jnp.transpose(update, (1, 0, 2)).reshape(columns, -1)
    accum = jnp.zeros((columns, sep_width), jnp.float32).at[:, targets.reshape(-1)].add(flat_update)
    piece = lax.psum_scatter(accum, "col", scatter_dimension=1, tiled=True)
    share = lax.psum(piece, ("leaf", "row"))
    reduced = (rhs_root.astype(jnp.float32) - share).astype(jnp.bfloat16)
    whole_reduced = lax.all_gather(reduced, "col", axis=1, tiled=True)
    y_root = jnp.dot(whole_reduced, dinv_root.T, preferred_element_type=jnp.float32).astype(
        jnp.bfloat16
    )
    return (solved[None], y_root)


def solution(mesh):
    in_specs = (
        P("leaf", None, None, "col"),
        P("leaf", None, "row", "col"),
        P("leaf", None, "col", "row"),
        P("leaf", None),
        P("leaf", None, None),
        P(None, "col"),
        P(("leaf", "row"), None),
    )
    out_specs = (P("leaf", None, None, "row"), P(None, ("leaf", "row")))
    return jax.shard_map(local, mesh=mesh, in_specs=in_specs, out_specs=out_specs, check_vma=False)
```

profile of v0, /device:TPU:0, one launch (start us, length us, event | category | flops | bytes accessed | tf_op | source)
XLA Modules:
  0.0 218.8 jit_solution(5079778243573968000)
XLA Ops:
  7.2 0.0 copy-start
  7.2 0.0 all-reduce.3.cloned.1.call-start
  7.2 0.9 compare_convert_fusion
  8.1 4.7 %fusion = f32[8,64,512]{2,1,0:T(8,128)} fusion(bf16[1,8,512,512]{3,2,1,0:T(8,128)(2,1)} %param.8, bf16[1,8,64,512]{3,2,1,0:T(8,128)(2,1)} %param.7, pred[8,512]{1,0:T(8,128)(4,1)S(1)} %get-tuple-element.3), kind=kOutput, calls=%fused_computation.1 | convolution fusion | flops 268697600 | bytes 5771264 | tf_op jit(solution)/shard_map/kbj,kij->kbi/dot_general | solution.py:16
  12.8 0.0 all-reduce.3.cloned.1.call-update
  12.8 0.0 reduce-scatter.2.cloned.1.call-start
  12.9 0.7 dynamic-slice_bitcast_fusion
  13.6 54.0 %all-reduce.3.cloned.1.call-done = f32[8,64,512]{2,1,0:T(8,128)} async-done(((f32[8,64,512]{2,1,0:T(8,128)}), f32[8,64,512]{2,1,0:T(8,128)}) %all-reduce.3.cloned.1.call-update) | async-done | bytes 1048592 | tf_op jit(solution)/shard_map/psum | solution.py:19
  67.6 0.0 copy-done
  67.6 2.0 fusion.4
  69.6 0.1 copy.13
  69.7 1.3 copy.12
  71.0 0.0 copy-start.2
  71.0 0.0 copy-start.1
  71.0 13.3 %scatter_custom_fusion = f32[64,4096]{0,1:T(8,128)} fusion(s32[2048]{0:T(1024)S(1)} %bitcast.29, f32[2048,64]{1,0:T(8,128)} %copy.12, f32[]{:T(128)} %constant.7.clone.1), kind=kCustom, calls=%fused_computation.7 | custom fusion | flops 131072 | bytes 1049088 | tf_op jit(solution)/shard_map/scatter-add | solution.py:27
  84.3 0.0 reduce-scatter.2.cloned.1.call-update
  84.3 0.0 all-reduce.5.cloned.1.call-start
  84.4 0.0 copy-done.2
  84.4 0.2 copy.10
  84.6 42.8 %reduce-scatter.2.cloned.1.call-done = f32[64,1024]{0,1:T(8,128)} async-done(((f32[64,4096]{0,1:T(8,128)}), f32[64,1024]{0,1:T(8,128)}) %reduce-scatter.2.cloned.1.call-update) | async-done | bytes 262160 | tf_op jit(solution)/shard_map/reduce_scatter | solution.py:28
  127.4 0.0 all-reduce.5.cloned.1.call-update
  127.4 0.0 copy-done.1
  127.4 0.9 fusion.11
  128.4 56.2 %all-reduce.5.cloned.1.call-done = f32[64,1024]{0,1:T(8,128)} async-done(((f32[64,1024]{0,1:T(8,128)}), f32[64,1024]{0,1:T(8,128)}) %all-reduce.5.cloned.1.call-update) | async-done | bytes 262160 | tf_op jit(solution)/shard_map/psum | solution.py:29
  184.5 1.1 subtract_convert_fusion
  185.6 22.4 %all_gather.3 = bf16[64,4096]{0,1:T(8,128)(2,1)S(1)} all-gather(bf16[64,1024]{0,1:T(8,128)(2,1)S(1)} %subtract_convert_fusion), channel_id=1, replica_groups=mesh['leaf'=2,'row'=4,'col'=4] {'col'}, dimensions={1}, use_global_device_ids=true | all-gather | bytes 655360 | tf_op jit(solution)/shard_map/all_gather | solution.py:31
  208.0 4.2 %convolution_convert_fusion = bf16[64,512]{1,0:T(8,128)(2,1)} fusion(bf16[64,4096]{0,1:T(8,128)(2,1)S(1)} %all_gather.3, bf16[512,4096]{1,0:T(8,128)(2,1)} %param.13), kind=kOutput, calls=%fused_computation.6 | convolution fusion | flops 268468224 | bytes 4784128 | tf_op jit(solution)/shard_map/dot_general | solution.py:32
  (3 shorter events, 0.0 us)
Async XLA Ops:
  7.2 60.5 %copy-start = (bf16[1,8,256,512]{3,2,1,0:T(8,128)(2,1)S(1)}, bf16[1,8,256,512]{3,2,1,0:T(8,128)(2,1)}, u32[]{:S(2)}) copy-start(bf16[1,8,256,512]{3,2,1,0:T(8,128)(2,1)} %param.9) | copy-start | bytes 6291460
  7.2 60.4 %all-reduce.3.cloned.1.call-start = ((), (), s32[]{:S(2)}) async-start(), calls=%async_computation.1 | async-start | bytes 2097152 | tf_op jit(solution)/shard_map/psum | solution.py:19
  12.8 114.6 %reduce-scatter.2.cloned.1.call-start = ((), (), s32[]{:S(2)}) async-start(), calls=%async_computation.2 | async-start | bytes 2621440 | tf_op jit(solution)/shard_map/reduce_scatter | solution.py:28
  71.0 13.4 %copy-start.2 = (bf16[64,1024]{1,0:T(8,128)(2,1)S(1)}, bf16[64,1024]{1,0:T(8,128)(2,1)}, u32[]{:S(2)}) copy-start(bf16[64,1024]{1,0:T(8,128)(2,1)} %param.12) | copy-start | bytes 393220
  71.0 56.5 %copy-start.1 = (f32[8,64,512]{2,1,0:T(8,128)S(1)}, f32[8,64,512]{2,1,0:T(8,128)}, u32[]{:S(2)}) copy-start(f32[8,64,512]{2,1,0:T(8,128)} %all-reduce.3.cloned.1.call-done) | copy-start | bytes 3145732
  84.3 100.2 %all-reduce.5.cloned.1.call-start = ((), (), s32[]{:S(2)}) async-start(), calls=%async_computation.3 | async-start | bytes 1048576 | tf_op jit(solution)/shard_map/psum | solution.py:29
Sparse Core Ops, SparseCore 0:
  13.0 54.6 all-reduce.2
  84.5 42.8 reduce-scatter.1
  130.5 53.9 all-reduce.4
where the time goes:
time: 219 us
  waiting for transfers between devices  153 us (70%)
  blocking collectives  22.4 us (10%)
  other arithmetic  16.2 us (7%)
  between operations  13.8 us (6%)
  matrix products  10.9 us (5%)
  local copies, waits for them, and re-layouts  2.27 us (1%)
    psum x1, waiting for transfers between devices, local(): share = lax.psum(piece, ('leaf', 'row'))  56.2 us
    psum x1, waiting for transfers between devices, local(): summed = lax.psum(partial_value, 'col')  54 us
    reduce_scatter x1, waiting for transfers between devices, local(): piece = lax.psum_scatter(accum, 'col', scatter_dimension=1, tiled=True)  42.8 us
    all_gather x1, blocking collectives, local(): whole_reduced = lax.all_gather(reduced, 'col', axis=1, tiled=True)  22.4 us
    scatter-add x1, other arithmetic, local(): jnp.zeros((columns, sep_width), jnp.float32).at[:, targets.reshape(-1)]  13.3 us
    dot_general x1, matrix products, local(): jnp.einsum('kbj,kij->kbi', masked, dinv_leaf[0], preferred_element_type=j...  4.71 us
  transfers between devices with their start and end apart: 3, of which 3 were waited for; matrix products, arithmetic and copies ran while one was open for 1% of the time, Pallas kernels for 0%

commit v1 on v0

--- a/solution.py
+++ b/solution.py
@@ -16,7 +16,9 @@
     partial_value = jnp.einsum(
         "kbj,kij->kbi", masked, dinv_leaf[0], preferred_element_type=jnp.float32
     )
-    summed = lax.psum(partial_value, "col")
+    summed = partial_value
+    for hop in (1, 2):
+        summed = summed + lax.ppermute(summed, "col", [(dev, dev ^ hop) for dev in range(4)])
     row_slots = lax.axis_index("row") * width_row + lax.iota(jnp.int32, width_row)
     live_rows = (row_slots[None, None, :] < limit).astype(jnp.float32)
     solved = (summed * live_rows).astype(jnp.bfloat16)

time: 219 us -> 240 us (1.096)
  waiting for transfers between devices: 153 us -> 169 us
  starting transfers between devices: 0.12 us -> 6.01 us
    ppermute x0 -> x2, waiting for transfers between devices: none -> 67.5 us  [local(): lax.ppermute(summed, 'col', [(dev, dev ^ hop) for dev in range(4)])]
    psum x1 -> x0, waiting for transfers between devices: 54 us -> none  [local(): summed = lax.psum(partial_value, 'col')]
    ppermute x0 -> x2, starting transfers between devices: none -> 5.93 us  [local(): lax.ppermute(summed, 'col', [(dev, dev ^ hop) for dev in range(4)])]
  transfers between devices with their start and end apart: 3 -> 4, of which waited for: 3 -> 4; matrix products, arithmetic and copies ran while one was open for 1% -> 0% of each run, Pallas kernels for 0% -> 0%
where the time goes in v1:
time: 240 us
  waiting for transfers between devices  169 us (70%)
  blocking collectives  22.4 us (9%)
  other arithmetic  16.9 us (7%)
  between operations  14.1 us (6%)
  matrix products  8.72 us (4%)
  starting transfers between devices  6.01 us (3%)
    ppermute x2, waiting for transfers between devices, local(): lax.ppermute(summed, 'col', [(dev, dev ^ hop) for dev in range(4)])  67.5 us
    psum x1, waiting for transfers between devices, local(): share = lax.psum(piece, ('leaf', 'row'))  56.9 us
    reduce_scatter x1, waiting for transfers between devices, local(): piece = lax.psum_scatter(accum, 'col', scatter_dimension=1, tiled=True)  44.7 us
    all_gather x1, blocking collectives, local(): whole_reduced = lax.all_gather(reduced, 'col', axis=1, tiled=True)  22.4 us
    scatter-add x1, other arithmetic, local(): jnp.zeros((columns, sep_width), jnp.float32).at[:, targets.reshape(-1)]  13.2 us
    ppermute x2, starting transfers between devices, local(): lax.ppermute(summed, 'col', [(dev, dev ^ hop) for dev in range(4)])  5.93 us
  transfers between devices with their start and end apart: 4, of which 4 were waited for; matrix products, arithmetic and copies ran while one was open for 0% of the time, Pallas kernels for 0%

profile of v1, /device:TPU:0, one launch (start us, length us, event | category | flops | bytes accessed | tf_op | source)
XLA Modules:
  0.0 239.6 jit_solution(15204526729501126434)
XLA Ops:
  7.2 0.0 copy-start
  7.2 0.0 reduce-scatter.2.cloned.1.call-start
  7.2 0.9 compare_convert_fusion
  8.1 3.7 %fusion = f32[8,64,512]{2,1,0:T(8,128)S(1)} fusion(bf16[1,8,512,512]{3,2,1,0:T(8,128)(2,1)} %param.8, bf16[1,8,64,512]{3,2,1,0:T(8,128)(2,1)} %param.7, pred[8,512]{1,0:T(8,128)(4,1)S(1)} %get-tuple-element.3), kind=kOutput, calls=%fused_computation.1 | convolution fusion | flops 268697600 | bytes 5771264 | tf_op jit(solution)/shard_map/kbj,kij->kbi/dot_general | solution.py:16
  11.8 3.1 %collective-permute-start = (f32[8,64,512]{2,1,0:T(8,128)S(1)}, f32[8,64,512]{2,1,0:T(8,128)S(1)}, u32[]{:S(2)}, u32[]{:S(2)}) collective-permute-start(f32[8,64,512]{2,1,0:T(8,128)S(1)} %fusion), channel_id=1, source_target_pairs={{0,1},{1,0},{2,3},{3,2},{4,5},{5,4},{6,7},{7,6},{8,9},{9,8},{10,11... | collective-permute-start | bytes 3145736 | tf_op jit(solution)/shard_map/ppermute | solution.py:21
  15.0 23.2 %collective-permute-done = f32[8,64,512]{2,1,0:T(8,128)S(1)} collective-permute-done((f32[8,64,512]{2,1,0:T(8,128)S(1)}, f32[8,64,512]{2,1,0:T(8,128)S(1)}, u32[]{:S(2)}, u32[]{:S(2)}) %collective-permute-start) | collective-permute-done | bytes 1048608 | tf_op jit(solution)/shard_map/ppermute | solution.py:21
  38.1 0.2 add.50
  38.3 2.8 %collective-permute-start.1 = (f32[8,64,512]{2,1,0:T(8,128)S(1)}, f32[8,64,512]{2,1,0:T(8,128)}, u32[]{:S(2)}, u32[]{:S(2)}) collective-permute-start(f32[8,64,512]{2,1,0:T(8,128)S(1)} %add.50), channel_id=1, source_target_pairs={{0,2},{1,3},{2,0},{3,1},{4,6},{5,7},{6,4},{7,5},{8,10},{9,11},{10,... | collective-permute-start | bytes 3145736 | tf_op jit(solution)/shard_map/ppermute | solution.py:21
  41.1 0.7 dynamic-slice_bitcast_fusion
  41.9 44.3 %collective-permute-done.1 = f32[8,64,512]{2,1,0:T(8,128)} collective-permute-done((f32[8,64,512]{2,1,0:T(8,128)S(1)}, f32[8,64,512]{2,1,0:T(8,128)}, u32[]{:S(2)}, u32[]{:S(2)}) %collective-permute-start.1) | collective-permute-done | bytes 1048608 | tf_op jit(solution)/shard_map/ppermute | solution.py:21
  86.2 1.5 multiply_convert_fusion
  87.7 0.0 copy-done
  87.7 0.0 copy-start.1
  87.7 0.8 fusion.4
  88.5 0.0 copy-done.1
  88.5 1.3 copy.12
  89.8 0.0 copy-start.2
  89.8 13.2 %scatter_custom_fusion = f32[64,4096]{0,1:T(8,128)} fusion(s32[2048]{0:T(1024)S(1)} %bitcast.30, f32[2048,64]{1,0:T(8,128)} %copy.12, f32[]{:T(128)} %constant.7.clone.1), kind=kCustom, calls=%fused_computation.7 | custom fusion | flops 131072 | bytes 1049088 | tf_op jit(solution)/shard_map/scatter-add | solution.py:29
  103.1 0.0 reduce-scatter.2.cloned.1.call-update
  103.1 0.0 all-reduce.2.cloned.1.call-start
  103.2 44.7 %reduce-scatter.2.cloned.1.call-done = f32[64,1024]{0,1:T(8,128)} async-done(((f32[64,4096]{0,1:T(8,128)}), f32[64,1024]{0,1:T(8,128)}) %reduce-scatter.2.cloned.1.call-update) | async-done | bytes 262160 | tf_op jit(solution)/shard_map/reduce_scatter | solution.py:30
  147.9 0.0 all-reduce.2.cloned.1.call-update
  147.9 0.0 copy-done.2
  147.9 0.2 copy.10
  148.1 56.9 %all-reduce.2.cloned.1.call-done = f32[64,1024]{0,1:T(8,128)} async-done(((f32[64,1024]{0,1:T(8,128)}), f32[64,1024]{0,1:T(8,128)}) %all-reduce.2.cloned.1.call-update) | async-done | bytes 262160 | tf_op jit(solution)/shard_map/psum | solution.py:31
  205.0 1.1 subtract_convert_fusion
  206.1 22.4 %all_gather.3 = bf16[64,4096]{0,1:T(8,128)(2,1)S(1)} all-gather(bf16[64,1024]{0,1:T(8,128)(2,1)S(1)} %subtract_convert_fusion), channel_id=1, replica_groups=mesh['leaf'=2,'row'=4,'col'=4] {'col'}, dimensions={1}, use_global_device_ids=true | all-gather | bytes 655360 | tf_op jit(solution)/shard_map/all_gather | solution.py:33
  228.5 4.2 %convolution_convert_fusion = bf16[64,512]{1,0:T(8,128)(2,1)} fusion(bf16[64,4096]{0,1:T(8,128)(2,1)S(1)} %all_gather.3, bf16[512,4096]{1,0:T(8,128)(2,1)} %param.13), kind=kOutput, calls=%fused_computation.6 | convolution fusion | flops 268468224 | bytes 4784128 | tf_op jit(solution)/shard_map/dot_general | solution.py:34
  (4 shorter events, 0.1 us)
Async XLA Ops:
  7.2 80.5 %copy-start = (bf16[1,8,256,512]{3,2,1,0:T(8,128)(2,1)S(1)}, bf16[1,8,256,512]{3,2,1,0:T(8,128)(2,1)}, u32[]{:S(2)}) copy-start(bf16[1,8,256,512]{3,2,1,0:T(8,128)(2,1)} %param.9) | copy-start | bytes 6291460
  7.2 140.7 %reduce-scatter.2.cloned.1.call-start = ((), (), s32[]{:S(2)}) async-start(), calls=%async_computation.1 | async-start | bytes 2621440 | tf_op jit(solution)/shard_map/reduce_scatter | solution.py:30
  11.8 26.3 %collective-permute-start = (f32[8,64,512]{2,1,0:T(8,128)S(1)}, f32[8,64,512]{2,1,0:T(8,128)S(1)}, u32[]{:S(2)}, u32[]{:S(2)}) collective-permute-start(f32[8,64,512]{2,1,0:T(8,128)S(1)} %fusion), channel_id=1, source_target_pairs={{0,1},{1,0},{2,3},{3,2},{4,5},{5,4},{6,7},{7,6},{8,9},{9,8},{10,11... | collective-permute-start | bytes 3145736 | tf_op jit(solution)/shard_map/ppermute | solution.py:21
  38.3 47.9 %collective-permute-start.1 = (f32[8,64,512]{2,1,0:T(8,128)S(1)}, f32[8,64,512]{2,1,0:T(8,128)}, u32[]{:S(2)}, u32[]{:S(2)}) collective-permute-start(f32[8,64,512]{2,1,0:T(8,128)S(1)} %add.50), channel_id=1, source_target_pairs={{0,2},{1,3},{2,0},{3,1},{4,6},{5,7},{6,4},{7,5},{8,10},{9,11},{10,... | collective-permute-start | bytes 3145736 | tf_op jit(solution)/shard_map/ppermute | solution.py:21
  87.7 0.8 copy-start.1
  89.8 58.1 %copy-start.2 = (bf16[64,1024]{1,0:T(8,128)(2,1)S(1)}, bf16[64,1024]{1,0:T(8,128)(2,1)}, u32[]{:S(2)}) copy-start(bf16[64,1024]{1,0:T(8,128)(2,1)} %param.12) | copy-start | bytes 393220
  103.1 101.9 %all-reduce.2.cloned.1.call-start = ((), (), s32[]{:S(2)}) async-start(), calls=%async_computation.2 | async-start | bytes 1048576 | tf_op jit(solution)/shard_map/psum | solution.py:31
Sparse Core Ops, SparseCore 0:
  103.2 44.6 reduce-scatter.1
  151.0 53.9 all-reduce.1
